TPU v7x, 32 devices: a whole 2x2x4 slice. The times are simulated.
32 devices in a mesh: groups: 2 (over x), seq: 16 (over z, y, core).
Axes of the slice: x: 2, y: 2, z: 4, core: 2. Of those that a mesh axis runs over, the one named last changes fastest.
Arguments:
- query_block: bfloat16 [512, 4096], P(('groups', 'seq')), parts along dimension 0, may hold values from -112 to 112
- cache_keys: bfloat16 [8192, 2048], P(('groups', 'seq')), parts along dimension 0, may hold values from -4 to 4
- stored_values: bfloat16 [8192, 2048], P(('groups', 'seq')), parts along dimension 0, may hold values from -6 to 6
- live_counts: int32 [32], P(('groups', 'seq')), parts along dimension 0, may hold values from 128 to 256
- first_position: int32 [2], P('groups'), parts along dimension 0, may hold values from 0 to 3840
- out_weight: bfloat16 [4096, 5376], P('seq'), may hold values from -0.09375 to 0.09375
Outputs:
- attended: bfloat16 [512, 5376], P(('groups', 'seq')), parts along dimension 0
There are 2 independent parts, one for each index of `groups`. A program takes and returns all parts, laid end to end along the dimension named above; an argument that names none is the same for every part. Nothing has to cross between parts.
Inputs may be any that keep to these rules, and one draw needn't show every extreme that they name: `live_counts`: the live slots of a block are its first ones.
All inputs are finite; a program needn't handle non-finite values.
Results may differ from a plain program's by a relative error of at most 0.0058.
Values may be sent and summed in bfloat16 or wider, within the bound.
No kernel may reach another device: no remote copies, remote signals or barrier semaphores. Data moves between devices by JAX's collectives and lax.ppermute only.
A program may use at most 64 MiB of HBM per device.

v0:
```python
import jax
import jax.numpy as jnp
from jax import lax
from jax.sharding import PartitionSpec as P

QUERY_HEADS = 32
KEY_VALUE_HEADS = 16
HEAD_SIZE = 128
score_scale = 168.0 ** (-0.5)
masked_value = -1e30


def head_partial(query_cols, key_cols, value_cols, allowed, group_width):
    row_count = query_cols.shape[0]
    grouped = query_cols.reshape(row_count, group_width, HEAD_SIZE)
    scores = (
        jnp.einsum("rgd,kd->grk", grouped, key_cols, preferred_element_type=jnp.float32)
        * score_scale
    )
    row_best = jnp.max(jnp.where(allowed[None], scores, masked_value), axis=2)
    shifted = jnp.where(allowed[None], scores - row_best[:, :, None], -jnp.inf)
    weights = jnp.exp(shifted)
    weight_sum = jnp.sum(weights, axis=2)
    safe_total = jnp.where(weight_sum > 0, weight_sum, 1.0)
    weighted = jnp.einsum(
        "grk,kd->grd", weights.astype(jnp.bfloat16), value_cols, preferred_element_type=jnp.float32
    )
    value_partial_sum = (weighted / safe_total[:, :, None]).astype(jnp.bfloat16)
    log_sum_exp = jnp.where(weight_sum > 0, row_best + jnp.log(safe_total), masked_value)
    return (value_partial_sum, log_sum_exp)


def merge_sources(received, totals):
    largest = jnp.max(totals, axis=0)
    scales = jnp.exp(totals - largest[None])
    blended = jnp.sum(scales[..., None] * received.astype(jnp.float32), axis=0)
    return (blended / jnp.sum(scales, axis=0)[..., None]).astype(jnp.bfloat16)


def body(query_block, cache_keys, stored_values, live_counts, first_position, out_weight):
    devices = lax.axis_size("seq")
    source = lax.axis_index("seq")
    key_count = cache_keys.shape[0]
    row_total = query_block.shape[0] * devices
    per_group = QUERY_HEADS // devices
    group_width = QUERY_HEADS // KEY_VALUE_HEADS
    first_key = source * key_count
    live_count = live_counts[0]
    begin_pos = first_position[0]
    key_index = lax.iota(jnp.int32, key_count)
    piece_rows = lax.all_gather(query_block, "seq", axis=0, tiled=True)
    row_count = piece_rows.shape[0]
    query_pos = begin_pos + lax.iota(jnp.int32, row_count)
    allowed = (key_index[None, :] < live_count) & (
        first_key + key_index[None, :] <= query_pos[:, None]
    )

    def single_head(key_value_head):
        query_cols = lax.dynamic_slice_in_dim(
            piece_rows, key_value_head * (group_width * HEAD_SIZE), group_width * HEAD_SIZE, 1
        )
        key_cols = lax.dynamic_slice_in_dim(cache_keys, key_value_head * HEAD_SIZE, HEAD_SIZE, 1)
        value_cols = lax.dynamic_slice_in_dim(
            stored_values, key_value_head * HEAD_SIZE, HEAD_SIZE, 1
        )
        return head_partial(query_cols, key_cols, value_cols, allowed, group_width)

    value_partial_sum, log_sum_exp = lax.map(
        single_head, jnp.arange(KEY_VALUE_HEADS, dtype=jnp.int32)
    )
    value_partial_sum = jnp.transpose(value_partial_sum, (2, 0, 1, 3)).reshape(
        row_count, QUERY_HEADS, HEAD_SIZE
    )
    log_sum_exp = jnp.transpose(log_sum_exp, (2, 0, 1)).reshape(row_count, QUERY_HEADS)
    value_partial_sum, log_sum_exp = (value_partial_sum, log_sum_exp)
    value_partial_sum, log_sum_exp = (value_partial_sum, log_sum_exp)
    received = lax.all_to_all(
        value_partial_sum[None], "seq", split_axis=2, concat_axis=0, tiled=True
    )
    totals = lax.all_to_all(log_sum_exp[None], "seq", split_axis=2, concat_axis=0, tiled=True)
    merged = merge_sources(received, totals)
    flattened = merged.reshape(row_total, per_group * HEAD_SIZE)
    summed = lax.psum_scatter(
        jnp.dot(flattened, out_weight, preferred_element_type=jnp.float32),
        "seq",
        scatter_dimension=0,
        tiled=True,
    )
    return summed.astype(jnp.bfloat16)


def solution(mesh):
    in_specs = (
        P(("groups", "seq"), None),
        P(("groups", "seq"), None),
        P(("groups", "seq"), None),
        P(("groups", "seq")),
        P("groups"),
        P("seq", None),
    )
    out_specs = P(("groups", "seq"), None)
    return jax.shard_map(body, mesh=mesh, in_specs=in_specs, out_specs=out_specs, check_vma=False)
```

profile of v0, /device:TPU:0, one launch (start us, length us, event | category | flops | bytes accessed | tf_op | source)
XLA Modules:
  0.0 307.4 jit_solution(6038253713847439832)
XLA Ops:
  6.5 0.7 all-gather.2.cloned.1.call-update
  8.7 45.0 %all-gather.2.cloned.1.call-done = bf16[256,4096]{1,0:T(8,128)(2,1)} async-done(((bf16[16,4096]{1,0:T(8,128)(2,1)}), bf16[256,4096]{1,0:T(8,128)(2,1)}) %all-gather.2.cloned.1.call-update) | async-done | bytes 2097168 | tf_op jit(solution)/shard_map/all_gather | solution.py:51
  53.7 97.2 %while.13 = (s32[]{:T(128)}, bf16[16,2,256,128]{3,2,1,0:T(8,128)(2,1)}, f32[16,2,256]{2,1,0:T(2,128)S(1)}, s32[16]{0:T(128)S(1)}, bf16[256,2048]{1,0:T(8,128)(2,...) while((s32[]{:T(128)}, ...), condition=%wide.region_3.4_spmd.clone, body=%wide.region_0.3_spmd.clone.sunk | while | flops 68552712 | bytes 2775577 | solution.py:68
  53.7 0.6 dynamic_slice.35
  55.7 0.9 constant_dynamic-slice_fusion.2
  56.7 1.1 select_reduce_fusion.2
  58.0 1.8 fusion.40
  59.8 0.6 dynamic_slice.35
  61.8 0.9 constant_dynamic-slice_fusion.2
  62.8 1.1 select_reduce_fusion.2
  64.0 1.8 fusion.40
  65.9 0.6 dynamic_slice.35
  67.9 0.9 constant_dynamic-slice_fusion.2
  68.9 1.1 select_reduce_fusion.2
  70.1 1.8 fusion.40
  71.9 0.6 dynamic_slice.35
  73.9 0.9 constant_dynamic-slice_fusion.2
  75.0 1.1 select_reduce_fusion.2
  76.2 1.8 fusion.40
  78.0 0.6 dynamic_slice.35
  80.0 0.9 constant_dynamic-slice_fusion.2
  81.0 1.1 select_reduce_fusion.2
  82.3 1.8 fusion.40
  84.1 0.6 dynamic_slice.35
  86.1 0.9 constant_dynamic-slice_fusion.2
  87.1 1.1 select_reduce_fusion.2
  88.3 1.8 fusion.40
  92.1 0.9 constant_dynamic-slice_fusion.2
  93.2 1.1 select_reduce_fusion.2
  94.4 1.8 fusion.40
  98.2 0.9 constant_dynamic-slice_fusion.2
  99.2 1.1 select_reduce_fusion.2
  100.5 1.8 fusion.40
  104.3 0.9 constant_dynamic-slice_fusion.2
  105.3 1.1 select_reduce_fusion.2
  106.6 1.8 fusion.40
  110.4 0.9 constant_dynamic-slice_fusion.2
  111.4 1.1 select_reduce_fusion.2
  112.6 1.8 fusion.40
  116.5 0.9 constant_dynamic-slice_fusion.2
  117.5 1.1 select_reduce_fusion.2
  118.7 1.8 fusion.40
  122.5 0.9 constant_dynamic-slice_fusion.2
  123.6 1.1 select_reduce_fusion.2
  124.8 1.8 fusion.40
  128.6 0.9 constant_dynamic-slice_fusion.2
  129.7 1.1 select_reduce_fusion.2
  130.9 1.8 fusion.40
  134.7 0.9 constant_dynamic-slice_fusion.2
  135.7 1.1 select_reduce_fusion.2
  136.9 1.8 fusion.40
  140.8 0.9 constant_dynamic-slice_fusion.2
  141.8 1.1 select_reduce_fusion.2
  143.0 1.8 fusion.40
  146.8 0.9 constant_dynamic-slice_fusion.2
  147.8 1.1 select_reduce_fusion.2
  149.1 1.8 fusion.40
  151.0 9.9 %all_to_all.27 = f32[1,256,32]{1,0,2:T(1,128)S(1)} all-to-all(f32[1,256,32]{1,0,2:T(1,128)S(1)} %broadcast_in_dim_reshape.6), channel_id=1, replica_groups=mesh['groups'=2,'seq'=16] {'seq'}, dimensions={2} | all-to-all | bytes 65536 | tf_op jit(solution)/shard_map/all_to_all | solution.py:80
  160.8 4.4 %all-to-all-start.1 = ((bf16[1,256,32,128]{3,1,0,2:T(8,128)(2,1)}), bf16[1,256,32,128]{3,1,0,2:T(8,128)(2,1)}, u32[]{:S(2)}, u32[]{:S(2)}) async-start(bf16[1,256,32,128]{3,1,0,2:T(8,128)(2,1)} %bitcast.71), calls=%async_computation.1 | async-start | bytes 4194304 | tf_op jit(solution)/shard_map/all_to_all | solution.py:77
  165.4 40.8 %all-to-all-done.1 = bf16[1,256,32,128]{3,1,0,2:T(8,128)(2,1)} async-done(((bf16[1,256,32,128]{3,1,0,2:T(8,128)(2,1)}), bf16[1,256,32,128]{3,1,0,2:T(8,128)(2,1)}, u32[]{:S(2)}, u32[]{:S(2)}) %all-to-all-start.1) | async-done | bytes 2097184 | tf_op jit(solution)/shard_map/all_to_all | solution.py:77
  206.2 2.5 fusion.22
  209.0 3.3 %fusion.26 = f32[256,5376]{1,0:T(8,128)} fusion(bf16[256,256]{0,1:T(8,128)(2,1)S(1)} %bitcast.72, bf16[256,5376]{1,0:T(8,128)(2,1)S(1)} %copy-done), kind=kOutput, calls=%fused_computation.39 | convolution fusion | flops 704643072 | bytes 8388608 | tf_op jit(solution)/shard_map/dot_general | solution.py:84
  212.4 86.6 %reduce-scatter.2.cloned.1.call-done = f32[16,5376]{1,0:T(8,128)} async-done(((f32[256,5376]{1,0:T(8,128)}), f32[16,5376]{1,0:T(8,128)}) %reduce-scatter.2.cloned.1.call-update) | async-done | bytes 344080 | tf_op jit(solution)/shard_map/reduce_scatter | solution.py:83
  298.9 1.7 convert_element_type.34
  (105 shorter events, 12.6 us)
Async XLA Ops:
  6.5 202.5 %copy-start = (bf16[256,5376]{1,0:T(8,128)(2,1)S(1)}, bf16[256,5376]{1,0:T(8,128)(2,1)}, u32[]{:S(2)}) copy-start(bf16[256,5376]{1,0:T(8,128)(2,1)} %param.13) | copy-start | bytes 8257540
  6.5 47.2 %all-gather.2.cloned.1.call-start = ((), (), s32[]{:S(2)}) async-start(), calls=%async_computation.3 | async-start | bytes 2228224 | tf_op jit(solution)/shard_map/all_gather | solution.py:51
  160.8 45.4 %all-to-all-start.1 = ((bf16[1,256,32,128]{3,1,0,2:T(8,128)(2,1)}), bf16[1,256,32,128]{3,1,0,2:T(8,128)(2,1)}, u32[]{:S(2)}, u32[]{:S(2)}) async-start(bf16[1,256,32,128]{3,1,0,2:T(8,128)(2,1)} %bitcast.71), calls=%async_computation.1 | async-start | bytes 4194304 | tf_op jit(solution)/shard_map/all_to_all | solution.py:77
  165.3 133.6 %reduce-scatter.2.cloned.1.call-start = ((), (), s32[]{:S(2)}) async-start(), calls=%async_computation.4 | async-start | bytes 5849088 | tf_op jit(solution)/shard_map/reduce_scatter | solution.py:83
Sparse Core Ops, SparseCore 0:
  9.5 44.1 all-gather.1
  212.5 86.3 reduce-scatter.1
where the time goes:
time: 310 us; the launch traced here: 307 us
  waiting for transfers between devices  173 us (56%)
  matrix products  49.7 us (16%)
  local copies, waits for them, and re-layouts  25.9 us (8%)
  loops' own time  20.5 us (7%)
  between operations  14.9 us (5%)
  blocking collectives  9.87 us (3%)
  other arithmetic  9 us (3%)
  starting transfers between devices  4.47 us (1%)
    reduce_scatter x1, waiting for transfers between devices, body(): lax.psum_scatter(jnp.dot(flattened, out_weight, preferred_element_type=jn...  86.6 us
    all_gather x1, waiting for transfers between devices, body(): piece_rows = lax.all_gather(query_block, 'seq', axis=0, tiled=True)  45 us
    all_to_all x1, waiting for transfers between devices, body(): lax.all_to_all(value_partial_sum[None], 'seq', split_axis=2, concat_axis=...  40.8 us
    dot_general x16, matrix products, head_partial(): jnp.einsum('grk,kd->grd', weights.astype(jnp.bfloat16), value_cols, prefe...  29.2 us
    another operation x1, loops' own time, body(): lax.map(single_head, jnp.arange(KEY_VALUE_HEADS, dtype=jnp.int32))  20.5 us
    dot_general x16, matrix products, head_partial(): jnp.einsum('rgd,kd->grk', grouped, key_cols, preferred_element_type=jnp.f...  17.1 us
    dynamic_slice x32, local copies, waits for them, and re-layouts, single_head(): lax.dynamic_slice_in_dim(piece_rows, key_value_head * (group_width * HEAD...  16.3 us
    all_to_all x1, blocking collectives, body(): lax.all_to_all(log_sum_exp[None], 'seq', split_axis=2, concat_axis=0, til...  9.87 us
  transfers between devices with their start and end apart: 3, of which 3 were waited for; matrix products, arithmetic and copies ran while one was open for 0% of the time, Pallas kernels for 0%

commit v1 on v0

--- a/solution.py
+++ b/solution.py
@@ -74,8 +74,11 @@
     log_sum_exp = jnp.transpose(log_sum_exp, (2, 0, 1)).reshape(row_count, QUERY_HEADS)
     value_partial_sum, log_sum_exp = (value_partial_sum, log_sum_exp)
     value_partial_sum, log_sum_exp = (value_partial_sum, log_sum_exp)
-    received = lax.all_to_all(
-        value_partial_sum[None], "seq", split_axis=2, concat_axis=0, tiled=True
+    received = jnp.concatenate(
+        lax.all_to_all(
+            jnp.stack(jnp.split(value_partial_sum[None], lax.axis_size("seq"), axis=2)), "seq", 0, 0
+        ),
+        axis=0,
     )
     totals = lax.all_to_all(log_sum_exp[None], "seq", split_axis=2, concat_axis=0, tiled=True)
     merged = merge_sources(received, totals)

time: 310 us -> 324 us (1.045)
  local copies, waits for them, and re-layouts: 25.9 us -> 44.4 us
  blocking collectives: 9.87 us -> 0 us
  starting transfers between devices: 4.47 us -> 9.56 us
    unnamed x2 -> x19, local copies, waits for them, and re-layouts: 0.01 us -> 17.2 us
    all_to_all x1 -> x0, blocking collectives: 9.87 us -> none  [body(): lax.all_to_all(log_sum_exp[None], 'seq', split_axis=2, concat_axis=0, til...]
    all_to_all x1 -> x2, starting transfers between devices: 4.42 us -> 9.52 us  [the longest x1 6.02 us: body(): lax.all_to_all(jnp.stack(jnp.split(value_partial_sum[None], lax.axis_size...]
    all_to_all x1 -> x2, waiting for transfers between devices: 40.8 us -> 40.9 us  [the longest x1 40.9 us: body(): lax.all_to_all(jnp.stack(jnp.split(value_partial_sum[None], lax.axis_size...]
  transfers between devices with their start and end apart: 3 -> 4, of which waited for: 3 -> 3; matrix products, arithmetic and copies ran while one was open for 0% -> 6% of each run, Pallas kernels for 0% -> 0%
where the time goes in v1:
time: 324 us; the launch traced here: 321 us
  waiting for transfers between devices  173 us (53%)
  matrix products  49.7 us (15%)
  local copies, waits for them, and re-layouts  44.4 us (14%)
  loops' own time  20.5 us (6%)
  between operations  14.9 us (5%)
  starting transfers between devices  9.56 us (3%)
  other arithmetic  9 us (3%)
    reduce_scatter x1, waiting for transfers between devices, body(): lax.psum_scatter(jnp.dot(flattened, out_weight, preferred_element_type=jn...  86.6 us
    all_gather x1, waiting for transfers between devices, body(): piece_rows = lax.all_gather(query_block, 'seq', axis=0, tiled=True)  45 us
    all_to_all x1, waiting for transfers between devices, body(): lax.all_to_all(jnp.stack(jnp.split(value_partial_sum[None], lax.axis_size...  40.9 us
    dot_general x16, matrix products, head_partial(): jnp.einsum('grk,kd->grd', weights.astype(jnp.bfloat16), value_cols, prefe...  29.3 us
    another operation x1, loops' own time, body(): lax.map(single_head, jnp.arange(KEY_VALUE_HEADS, dtype=jnp.int32))  20.5 us
    unnamed x19, local copies, waits for them, and re-layouts  17.2 us
    dot_general x16, matrix products, head_partial(): jnp.einsum('rgd,kd->grk', grouped, key_cols, preferred_element_type=jnp.f...  17.1 us
    dynamic_slice x32, local copies, waits for them, and re-layouts, single_head(): lax.dynamic_slice_in_dim(piece_rows, key_value_head * (group_width * HEAD...  16.3 us
  transfers between devices with their start and end apart: 4, of which 3 were waited for; matrix products, arithmetic and copies ran while one was open for 6% of the time, Pallas kernels for 0%

profile of v1, /device:TPU:0, one launch (start us, length us, event | category | flops | bytes accessed | tf_op | source)
XLA Modules:
  0.0 321.3 jit_solution(13580168559673217180)
XLA Ops:
  8.7 45.0 %all-gather.2.cloned.1.call-done = bf16[256,4096]{1,0:T(8,128)(2,1)} async-done(((bf16[16,4096]{1,0:T(8,128)(2,1)}), bf16[256,4096]{1,0:T(8,128)(2,1)}) %all-gather.2.cloned.1.call-update) | async-done | bytes 2097168 | tf_op jit(solution)/shard_map/all_gather | solution.py:51
  53.7 97.3 %while.13 = (s32[]{:T(128)}, bf16[16,2,256,128]{3,2,1,0:T(8,128)(2,1)}, f32[16,2,256]{2,1,0:T(2,128)S(1)}, s32[16]{0:T(128)S(1)}, bf16[256,2048]{1,0:T(8,128)(2,...) while((s32[]{:T(128)}, ...), condition=%wide.region_3.4_spmd.clone, body=%wide.region_0.3_spmd.clone.sunk | while | flops 68552712 | bytes 2775577 | solution.py:68
  55.7 0.9 constant_dynamic-slice_fusion.2
  56.7 1.1 select_reduce_fusion.2
  58.0 1.8 fusion.56
  61.8 0.9 constant_dynamic-slice_fusion.2
  62.8 1.1 select_reduce_fusion.2
  64.0 1.8 fusion.56
  67.8 0.9 constant_dynamic-slice_fusion.2
  68.9 1.1 select_reduce_fusion.2
  70.1 1.8 fusion.56
  73.9 0.9 constant_dynamic-slice_fusion.2
  75.0 1.1 select_reduce_fusion.2
  76.2 1.8 fusion.56
  80.0 0.9 constant_dynamic-slice_fusion.2
  81.1 1.1 select_reduce_fusion.2
  82.3 1.8 fusion.56
  86.1 0.9 constant_dynamic-slice_fusion.2
  87.1 1.1 select_reduce_fusion.2
  88.4 1.8 fusion.56
  92.2 0.9 constant_dynamic-slice_fusion.2
  93.2 1.1 select_reduce_fusion.2
  94.4 1.8 fusion.56
  98.2 0.9 constant_dynamic-slice_fusion.2
  99.3 1.1 select_reduce_fusion.2
  100.5 1.8 fusion.56
  104.3 0.9 constant_dynamic-slice_fusion.2
  105.4 1.1 select_reduce_fusion.2
  106.6 1.8 fusion.56
  110.4 0.9 constant_dynamic-slice_fusion.2
  111.4 1.1 select_reduce_fusion.2
  112.7 1.8 fusion.56
  116.5 0.9 constant_dynamic-slice_fusion.2
  117.5 1.1 select_reduce_fusion.2
  118.8 1.8 fusion.56
  122.6 0.9 constant_dynamic-slice_fusion.2
  123.6 1.1 select_reduce_fusion.2
  124.8 1.8 fusion.56
  128.6 0.9 constant_dynamic-slice_fusion.2
  129.7 1.1 select_reduce_fusion.2
  130.9 1.8 fusion.56
  134.7 0.9 constant_dynamic-slice_fusion.2
  135.8 1.1 select_reduce_fusion.2
  137.0 1.8 fusion.56
  140.8 0.9 constant_dynamic-slice_fusion.2
  141.8 1.1 select_reduce_fusion.2
  143.1 1.8 fusion.56
  147.9 1.1 select_reduce_fusion.2
  149.1 1.8 fusion.56
  151.6 3.5 %all-to-all-start = ((f32[1,256,32]{1,0,2:T(1,128)}), f32[1,256,32]{1,0,2:T(1,128)S(1)}, u32[]{:S(2)}, u32[]{:S(2)}) async-start(f32[1,256,32]{1,0,2:T(1,128)} %broadcast_in_dim_reshape.6), calls=%async_computation | async-start | bytes 65536 | tf_op jit(solution)/shard_map/all_to_all | solution.py:83
  155.1 1.7 fusion.38
  156.9 1.6 fusion.37
  158.4 1.6 fusion.36
  160.0 1.6 fusion.35
  161.5 1.6 fusion.34
  163.1 1.6 fusion.33
  164.7 1.6 fusion.32
  166.2 1.6 fusion.31
  173.0 6.0 %all-to-all-start.1 = ((bf16[16,1,256,2,128]{4,2,3,1,0:T(8,128)(2,1)}), bf16[16,1,256,2,128]{4,2,3,1,0:T(8,128)(2,1)}, u32[]{:S(2)}, u32[]{:S(2)}) async-start(bf16[16,1,256,2,128]{4,2,3,1,0:T(8,128)(2,1)} %fusion.23), calls=%async_computation.1 | async-start | bytes 4194304 | tf_op jit(solution)/shard_map/all_to_all | solution.py:78
  179.2 40.9 %all-to-all-done.1 = bf16[16,1,256,2,128]{4,2,3,1,0:T(8,128)(2,1)} async-done(((bf16[16,1,256,2,128]{4,2,3,1,0:T(8,128)(2,1)}), bf16[16,1,256,2,128]{4,2,3,1,0:T(8,128)(2,1)}, u32[]{:S(2)}, u32[]{:S(2)}) %all-to-all-start.1) | async-done | bytes 2097184 | tf_op jit(solution)/shard_map/all_to_all | solution.py:78
  220.1 2.5 fusion.22
  222.9 3.3 %fusion.42 = f32[256,5376]{1,0:T(8,128)} fusion(bf16[256,256]{0,1:T(8,128)(2,1)S(1)} %bitcast.146, bf16[256,5376]{1,0:T(8,128)(2,1)S(1)} %copy-done), kind=kOutput, calls=%fused_computation.71 | convolution fusion | flops 704643072 | bytes 8388608 | tf_op jit(solution)/shard_map/dot_general | solution.py:87
  226.2 86.6 %reduce-scatter.2.cloned.1.call-done = f32[16,5376]{1,0:T(8,128)} async-done(((f32[256,5376]{1,0:T(8,128)}), f32[16,5376]{1,0:T(8,128)}) %reduce-scatter.2.cloned.1.call-update) | async-done | bytes 344080 | tf_op jit(solution)/shard_map/reduce_scatter | solution.py:86
  312.8 1.7 convert_element_type.26
  (124 shorter events, 23.6 us)
Async XLA Ops:
  6.5 216.3 %copy-start = (bf16[256,5376]{1,0:T(8,128)(2,1)S(1)}, bf16[256,5376]{1,0:T(8,128)(2,1)}, u32[]{:S(2)}) copy-start(bf16[256,5376]{1,0:T(8,128)(2,1)} %param.13) | copy-start | bytes 8257540
  6.5 47.2 %all-gather.2.cloned.1.call-start = ((), (), s32[]{:S(2)}) async-start(), calls=%async_computation.3 | async-start | bytes 2228224 | tf_op jit(solution)/shard_map/all_gather | solution.py:51
  151.6 21.4 %all-to-all-start = ((f32[1,256,32]{1,0,2:T(1,128)}), f32[1,256,32]{1,0,2:T(1,128)S(1)}, u32[]{:S(2)}, u32[]{:S(2)}) async-start(f32[1,256,32]{1,0,2:T(1,128)} %broadcast_in_dim_reshape.6), calls=%async_computation | async-start | bytes 65536 | tf_op jit(solution)/shard_map/all_to_all | solution.py:83
  155.1 12.6 %copy-start.1 = (bf16[16,2,256,128]{3,2,1,0:T(8,128)(2,1)S(1)}, bf16[16,2,256,128]{3,2,1,0:T(8,128)(2,1)}, u32[]{:S(2)}) copy-start(bf16[16,2,256,128]{3,2,1,0:T(8,128)(2,1)} %get-tuple-element.49) | copy-start | bytes 6291460
  173.0 47.1 %all-to-all-start.1 = ((bf16[16,1,256,2,128]{4,2,3,1,0:T(8,128)(2,1)}), bf16[16,1,256,2,128]{4,2,3,1,0:T(8,128)(2,1)}, u32[]{:S(2)}, u32[]{:S(2)}) async-start(bf16[16,1,256,2,128]{4,2,3,1,0:T(8,128)(2,1)} %fusion.23), calls=%async_computation.1 | async-start | bytes 4194304 | tf_op jit(solution)/shard_map/all_to_all | solution.py:78
  179.1 133.8 %reduce-scatter.2.cloned.1.call-start = ((), (), s32[]{:S(2)}) async-start(), calls=%async_computation.4 | async-start | bytes 5849088 | tf_op jit(solution)/shard_map/reduce_scatter | solution.py:86
Sparse Core Ops, SparseCore 0:
  9.5 44.1 all-gather.1
  226.3 86.4 reduce-scatter.1
